TPU v7x, 32 devices: a whole 2x2x4 slice. The times are simulated.
32 devices in a mesh: occ: 2 (over x), vir: 4 (over z), aux: 4 (over y, core).
Axes of the slice: x: 2, y: 2, z: 4, core: 2. Of those that a mesh axis runs over, the one named last changes fastest.
Arguments:
- amplitudes: bfloat16 [16, 1024, 1024], P('occ', 'vir'), may hold values from -6 to 6
- pair_mask: int32 [16, 8, 8], P('occ', 'vir'), may hold values 0 or 1
- left_factor: bfloat16 [32, 1024, 4096], P(None, 'vir', 'aux'), may hold values from -0.0390625 to 0.0390625
- left_mask: int32 [8, 32], P('vir', 'aux'), may hold values 0 or 1
- right_factor: bfloat16 [1024, 4, 4096], P(('occ', 'vir'), None, 'aux'), may hold values from -0.0390625 to 0.0390625
- right_mask: int32 [8, 32], P(None, 'aux'), may hold values 0 or 1
- residual_in: float32 [16, 4, 32], P('occ'), may hold values from -6 to 6
Outputs:
- updated: float32 [16, 4, 32], P('occ')
All inputs are finite; a program needn't handle non-finite values. No bound on the sum of `pair_mask` or of `left_mask` or of `right_mask` on one device may be relied on, other than what follows from the above.
Results may differ from a plain program's by a relative error of at most 0.0003.
Values may be sent and summed in bfloat16 or wider, within the bound.
No kernel may reach another device: no remote copies, remote signals or barrier semaphores. Data moves between devices by JAX's collectives and lax.ppermute only.
A program may use at most 128 MiB of HBM per device.

v0:
```python
import jax
import jax.numpy as jnp
from jax import lax
from jax.sharding import PartitionSpec as P

TILE = 128


def expand_tiles(mask, width):
    return jnp.repeat(jnp.repeat(mask, width, axis=-2), width, axis=-1)


def local(amplitudes, pair_mask, left_factor, left_mask, right_factor, right_mask, residual_in):
    pairs_here, cols_here, virt_all = amplitudes.shape
    rows_here, block_b, aux_here = right_factor.shape
    tau = amplitudes * expand_tiles(pair_mask, TILE).astype(jnp.bfloat16)
    left = left_factor * expand_tiles(left_mask, TILE).astype(jnp.bfloat16)[None, :, :]
    tiles_all = right_mask.shape[0]
    aux_mask = jnp.repeat(right_mask, TILE, axis=1).astype(jnp.float32)
    row_start = lax.axis_index(("occ", "vir")) * rows_here
    row_tiles = (row_start + jnp.arange(rows_here, dtype=jnp.int32)) // TILE
    onehot = (row_tiles[:, None] == jnp.arange(tiles_all, dtype=jnp.int32)[None, :]).astype(
        jnp.float32
    )
    row_mask = jnp.dot(onehot, aux_mask, preferred_element_type=jnp.float32)
    right = right_factor * row_mask.astype(jnp.bfloat16)[:, None, :]
    right_whole = lax.all_gather(right, ("occ", "vir"), axis=0, tiled=True)
    tau_flat = tau.reshape(pairs_here * cols_here, virt_all)
    left_wide = left.astype(jnp.float32)
    columns = []
    for index_b in range(block_b):
        inner_b = jnp.dot(tau_flat, right_whole[:, index_b, :], preferred_element_type=jnp.float32)
        inner_b = inner_b.reshape(pairs_here, cols_here, aux_here)
        columns.append(
            jnp.einsum(
                "pcq,acq->pa",
                inner_b,
                left_wide,
                precision=lax.Precision.HIGHEST,
                preferred_element_type=jnp.float32,
            )
        )
    partial_sum = jnp.stack(columns, axis=1)
    total = lax.psum(partial_sum, ("vir", "aux"))
    return residual_in + total


def solution(mesh):
    return jax.shard_map(
        local,
        mesh=mesh,
        in_specs=(
            P("occ", "vir", None),
            P("occ", "vir", None),
            P(None, "vir", "aux"),
            P("vir", "aux"),
            P(("occ", "vir"), None, "aux"),
            P(None, "aux"),
            P("occ", None, None),
        ),
        out_specs=P("occ", None, None),
        check_vma=False,
    )
```

profile of v0, /device:TPU:0, one launch (start us, length us, event | category | flops | bytes accessed | tf_op | source)
XLA Modules:
  0.0 383.0 jit_solution(14707230647622306978)
XLA Ops:
  6.5 0.0 all-gather.2.cloned.1.call-start
  6.5 0.7 convert_element_type.41
  7.2 0.1 broadcast_bitcast_fusion
  7.3 0.3 convolution_convert_fusion
  7.6 0.0 copy-start.3
  7.6 3.0 copy_multiply_fusion
  10.6 0.0 all-gather.2.cloned.1.call-update
  10.6 0.7 convert_element_type.38
  11.3 0.1 broadcast_in_dim.19
  11.4 3.8 %broadcast_in_dim.20 = bf16[8,256,8,128]{3,2,1,0:T(8,128)(2,1)} broadcast(bf16[8,256,8]{2,1,0:T(8,128)(2,1)S(1)} %bitcast.46), dimensions={0,1,2} | broadcast | bytes 4227072 | tf_op jit(solution)/shard_map/broadcast_in_dim | solution.py:10
  15.2 7.4 %convert_element_type.40 = bf16[8,256,1024]{2,1,0:T(8,128)(2,1)} reshape(bf16[8,256,8,128]{3,2,1,0:T(8,128)(2,1)} %broadcast_in_dim.20) | data formatting | bytes 8388608 | tf_op jit(solution)/shard_map/convert_element_type | solution.py:16
  22.6 0.0 copy-done.3
  22.7 0.3 broadcast_in_dim.23
  23.0 0.1 copy.55
  23.1 7.9 %mul.25 = bf16[8,256,1024]{2,1,0:T(8,128)(2,1)} multiply(bf16[8,256,1024]{2,1,0:T(8,128)(2,1)} %param.7, bf16[8,256,1024]{2,1,0:T(8,128)(2,1)} %convert_element_type.40) | non-fusion elementwise | flops 2097152 | bytes 12582912 | tf_op jit(solution)/shard_map/mul | solution.py:16
  31.0 13.8 %broadcast_multiply_fusion = bf16[32,256,1024]{2,1,0:T(8,128)(2,1)} fusion(bf16[32,256,1024]{2,1,0:T(8,128)(2,1)} %param.9, bf16[256,1024]{1,0:T(8,128)(2,1)S(1)} %bitcast.45), kind=kLoop, calls=%fused_computation.8 | loop fusion | flops 8388608 | bytes 34078720 | tf_op jit(solution)/shard_map/mul | solution.py:17
  44.9 93.1 %all-gather.2.cloned.1.call-done = bf16[1024,4,1024]{2,0,1:T(8,128)(2,1)} async-done(((bf16[128,4,1024]{2,0,1:T(8,128)(2,1)}), bf16[1024,4,1024]{2,0,1:T(8,128)(2,1)}) %all-gather.2.cloned.1.call-update) | async-done | bytes 8388624 | tf_op jit(solution)/shard_map/all_gather | solution.py:27
  138.0 0.0 copy-start
  138.0 11.6 %fusion.14 = f32[8,256,1024]{2,0,1:T(8,128)} fusion(bf16[8,256,1024]{2,1,0:T(8,128)(2,1)} %mul.25, bf16[1024,4,1024]{2,0,1:T(8,128)(2,1)} %all-gather.2.cloned.1.call-done), kind=kOutput, calls=%fused_computation.15 | convolution fusion | flops 4294967296 | bytes 14680064 | tf_op jit(solution)/shard_map/dot_general | solution.py:32
  149.6 0.0 copy-done
  149.6 0.0 copy-start.1
  149.6 32.4 %fusion.16 = f32[8,1,32]{2,0,1:T(8,128)S(1)} fusion(f32[8,256,1024]{2,0,1:T(8,128)} %fusion.14, bf16[32,256,1024]{2,1,0:T(8,128)(2,1)S(1)} %copy-done), kind=kOutput, calls=%fused_computation.22 | convolution fusion | flops 805306368 | bytes 25166848 | tf_op jit(solution)/shard_map/pcq,acq->pa/dot_general | solution.py:35
  181.9 0.0 copy-done.1
  181.9 12.3 %fusion.12 = f32[8,256,1024]{2,0,1:T(8,128)} fusion(bf16[8,256,1024]{2,1,0:T(8,128)(2,1)S(1)} %copy-done.1, bf16[1024,4,1024]{2,0,1:T(8,128)(2,1)} %all-gather.2.cloned.1.call-done), kind=kOutput, calls=%fused_computation.13 | convolution fusion | flops 4294967296 | bytes 14680064 | tf_op jit(solution)/shard_map/dot_general | solution.py:32
  194.2 32.6 %fusion.19 = f32[8,1,32]{2,0,1:T(8,128)S(1)} fusion(f32[8,256,1024]{2,0,1:T(8,128)} %fusion.12, bf16[32,256,1024]{2,1,0:T(8,128)(2,1)S(1)} %copy-done), kind=kOutput, calls=%fused_computation.23 | convolution fusion | flops 805306368 | bytes 25166848 | tf_op jit(solution)/shard_map/pcq,acq->pa/dot_general | solution.py:35
  226.8 12.3 %fusion.10 = f32[8,256,1024]{2,0,1:T(8,128)} fusion(bf16[8,256,1024]{2,1,0:T(8,128)(2,1)S(1)} %copy-done.1, bf16[1024,4,1024]{2,0,1:T(8,128)(2,1)} %all-gather.2.cloned.1.call-done), kind=kOutput, calls=%fused_computation.11 | convolution fusion | flops 4294967296 | bytes 14680064 | tf_op jit(solution)/shard_map/dot_general | solution.py:32
  239.1 32.4 %fusion.22 = f32[8,1,32]{2,0,1:T(8,128)S(1)} fusion(f32[8,256,1024]{2,0,1:T(8,128)} %fusion.10, bf16[32,256,1024]{2,1,0:T(8,128)(2,1)S(1)} %copy-done), kind=kOutput, calls=%fused_computation.24 | convolution fusion | flops 805306368 | bytes 25166848 | tf_op jit(solution)/shard_map/pcq,acq->pa/dot_general | solution.py:35
  271.5 12.3 %fusion.8 = f32[8,256,1024]{2,0,1:T(8,128)} fusion(bf16[8,256,1024]{2,1,0:T(8,128)(2,1)S(1)} %copy-done.1, bf16[1024,4,1024]{2,0,1:T(8,128)(2,1)} %all-gather.2.cloned.1.call-done), kind=kOutput, calls=%fused_computation.9 | convolution fusion | flops 4294967296 | bytes 14680064 | tf_op jit(solution)/shard_map/dot_general | solution.py:32
  283.8 0.0 copy-start.2
  283.8 32.2 %fusion.25 = f32[8,1,32]{2,0,1:T(8,128)S(1)} fusion(f32[8,256,1024]{2,0,1:T(8,128)} %fusion.8, bf16[32,256,1024]{2,1,0:T(8,128)(2,1)S(1)} %copy-done), kind=kOutput, calls=%fused_computation.25 | convolution fusion | flops 805306368 | bytes 25166848 | tf_op jit(solution)/shard_map/pcq,acq->pa/dot_general | solution.py:35
  316.0 59.4 %psum.7 = f32[8,4,32]{2,0,1:T(8,128)S(1)} all-reduce(f32[8,4,32]{2,0,1:T(8,128)S(1)} %pad_maximum_fusion), channel_id=1, replica_groups=mesh['occ'=2,'vir'=4,'aux'=4] {'vir','aux'}, use_global_device_ids=true, to_apply=%region_0.1 | all-reduce | flops 1024 | bytes 8192 | tf_op jit(solution)/shard_map/psum | solution.py:44
  375.4 0.0 copy-done.2
  375.4 0.6 copy.20
  (5 shorter events, 0.0 us)
Async XLA Ops:
  6.5 131.4 %all-gather.2.cloned.1.call-start = ((), (), s32[]{:S(2)}) async-start(), calls=%async_computation | async-start | bytes 9437184 | tf_op jit(solution)/shard_map/all_gather | solution.py:27
  7.6 15.1 %copy-start.3 = (s32[2,8]{1,0:T(2,128)S(1)}, s32[2,8]{1,0:T(2,128)}, u32[]{:S(2)}) copy-start(s32[2,8]{1,0:T(2,128)} %param.10) | copy-start | bytes 196
  138.0 11.6 %copy-start = (bf16[32,256,1024]{2,1,0:T(8,128)(2,1)S(1)}, bf16[32,256,1024]{2,1,0:T(8,128)(2,1)}, u32[]{:S(2)}) copy-start(bf16[32,256,1024]{2,1,0:T(8,128)(2,1)} %broadcast_multiply_fusion) | copy-start | bytes 50331652
  149.6 32.4 %copy-start.1 = (bf16[8,256,1024]{2,1,0:T(8,128)(2,1)S(1)}, bf16[8,256,1024]{2,1,0:T(8,128)(2,1)}, u32[]{:S(2)}) copy-start(bf16[8,256,1024]{2,1,0:T(8,128)(2,1)} %mul.25) | copy-start | bytes 12582916
  283.8 91.6 %copy-start.2 = (f32[8,4,32]{2,1,0:T(4,128)S(1)}, f32[8,4,32]{2,1,0:T(4,128)}, u32[]{:S(2)}) copy-start(f32[8,4,32]{2,1,0:T(4,128)} %param.13) | copy-start | bytes 12292
Sparse Core Ops, SparseCore 0:
  10.7 127.1 all-gather.1
where the time goes:
time: 391 us; the launch traced here: 383 us
  matrix products  178 us (46%)
  waiting for transfers between devices  93.1 us (24%)
  blocking collectives  59.4 us (15%)
  other arithmetic  26.2 us (7%)
  between operations  13.6 us (3%)
  local copies, waits for them, and re-layouts  12.5 us (3%)
    dot_general x4, matrix products, local(): jnp.einsum('pcq,acq->pa', inner_b, left_wide, precision=lax.Precision.HIG...  130 us
    all_gather x1, waiting for transfers between devices, local(): right_whole = lax.all_gather(right, ('occ', 'vir'), axis=0, tiled=True)  93.1 us
    psum x1, blocking collectives, local(): total = lax.psum(partial_sum, ('vir', 'aux'))  59.4 us
    dot_general x4, matrix products, local(): jnp.dot(tau_flat, right_whole[:, index_b, :], preferred_element_type=jnp....  48.4 us
    mul x1, other arithmetic, local(): left_factor * expand_tiles(left_mask, TILE).astype(jnp.bfloat16)[None, :, :]  13.8 us
    mul x1, other arithmetic, local(): tau = amplitudes * expand_tiles(pair_mask, TILE).astype(jnp.bfloat16)  7.92 us
  transfers between devices with their start and end apart: 1, of which 1 were waited for; matrix products, arithmetic and copies ran while one was open for 9% of the time, Pallas kernels for 0%

commit v1 on v0

--- a/solution.py
+++ b/solution.py
@@ -24,7 +24,10 @@
     )
     row_mask = jnp.dot(onehot, aux_mask, preferred_element_type=jnp.float32)
     right = right_factor * row_mask.astype(jnp.bfloat16)[:, None, :]
-    right_whole = lax.all_gather(right, ("occ", "vir"), axis=0, tiled=True)
+    right_whole = jnp.concatenate(
+        lax.all_to_all(jnp.stack([right] * lax.axis_size(("occ", "vir"))), ("occ", "vir"), 0, 0),
+        axis=0,
+    )
     tau_flat = tau.reshape(pairs_here * cols_here, virt_all)
     left_wide = left.astype(jnp.float32)
     columns = []

time: 391 us -> 459 us (1.17)
  waiting for transfers between devices: 93.1 us -> 151 us
  between operations: 13.6 us -> 0.49 us
  local copies, waits for them, and re-layouts: 12.5 us -> 25.3 us
  starting transfers between devices: 0.01 us -> 7.42 us
  matrix products: 178 us -> 185 us
    all_to_all x0 -> x1, waiting for transfers between devices: none -> 151 us  [local(): lax.all_to_all(jnp.stack([right] * lax.axis_size(('occ', 'vir'))), ('occ'...]
    all_gather x1 -> x0, waiting for transfers between devices: 93.1 us -> none  [local(): right_whole = lax.all_gather(right, ('occ', 'vir'), axis=0, tiled=True)]
    dot_general x4, matrix products: 130 us -> 139 us  [local(): jnp.einsum('pcq,acq->pa', inner_b, left_wide, precision=lax.Precision.HIG...]
    all_to_all x0 -> x1, local copies, waits for them, and re-layouts: none -> 8.34 us  [local(): lax.all_to_all(jnp.stack([right] * lax.axis_size(('occ', 'vir'))), ('occ'...]
    all_to_all x0 -> x1, starting transfers between devices: none -> 7.42 us  [local(): lax.all_to_all(jnp.stack([right] * lax.axis_size(('occ', 'vir'))), ('occ'...]
  transfers between devices with their start and end apart: 1 -> 1, of which waited for: 1 -> 1; matrix products, arithmetic and copies ran while one was open for 9% -> 7% of each run, Pallas kernels for 0% -> 0%
where the time goes in v1:
time: 459 us; the launch traced here: 451 us
  matrix products  185 us (40%)
  waiting for transfers between devices  151 us (33%)
  blocking collectives  57.6 us (13%)
  local copies, waits for them, and re-layouts  25.3 us (6%)
  other arithmetic  24.2 us (5%)
  starting transfers between devices  7.42 us (2%)
    all_to_all x1, waiting for transfers between devices, local(): lax.all_to_all(jnp.stack([right] * lax.axis_size(('occ', 'vir'))), ('occ'...  151 us
    dot_general x4, matrix products, local(): jnp.einsum('pcq,acq->pa', inner_b, left_wide, precision=lax.Precision.HIG...  139 us
    psum x1, blocking collectives, local(): total = lax.psum(partial_sum, ('vir', 'aux'))  57.6 us
    dot_general x4, matrix products, local(): jnp.dot(tau_flat, right_whole[:, index_b, :], preferred_element_type=jnp....  45.9 us
    mul x1, other arithmetic, local(): left_factor * expand_tiles(left_mask, TILE).astype(jnp.bfloat16)[None, :, :]  13.8 us
  transfers between devices with their start and end apart: 1, of which 1 were waited for; matrix products, arithmetic and copies ran while one was open for 7% of the time, Pallas kernels for 0%

profile of v1, /device:TPU:0, one launch (start us, length us, event | category | flops | bytes accessed | tf_op | source)
XLA Modules:
  0.0 451.0 jit_solution(1037591159827580294)
XLA Ops:
  0.0 0.7 convert_element_type.41
  0.7 0.1 broadcast_bitcast_fusion
  0.8 0.3 convolution_convert_fusion
  1.1 1.8 broadcast_multiply_fusion.1
  2.9 0.3 copy.21
  3.2 4.3 stack.12
  7.5 0.0 copy-start.3
  7.5 7.4 %all-to-all-start = ((bf16[8,128,4,1024]{3,1,2,0:T(8,128)(2,1)}), bf16[8,128,4,1024]{3,1,2,0:T(8,128)(2,1)}, u32[]{:S(2)}, u32[]{:S(2)}) async-start(bf16[8,128,4,1024]{3,1,2,0:T(8,128)(2,1)} %stack.12), calls=%async_computation | async-start | bytes 16777216 | tf_op jit(solution)/shard_map/all_to_all | solution.py:28
  14.9 0.0 copy-done.3
  14.9 0.0 copy-start.4
  15.0 0.1 broadcast_in_dim.19
  15.0 3.8 broadcast_in_dim.20
  18.9 7.3 %convert_element_type.40 = bf16[8,256,1024]{2,1,0:T(8,128)(2,1)} reshape(bf16[8,256,8,128]{3,2,1,0:T(8,128)(2,1)} %broadcast_in_dim.20) | data formatting | bytes 8388608 | tf_op jit(solution)/shard_map/convert_element_type | solution.py:16
  26.2 0.0 copy-done.4
  26.2 0.3 broadcast_in_dim.23
  26.6 0.1 copy.65
  26.7 7.8 %mul.25 = bf16[8,256,1024]{2,1,0:T(8,128)(2,1)} multiply(bf16[8,256,1024]{2,1,0:T(8,128)(2,1)} %param.7, bf16[8,256,1024]{2,1,0:T(8,128)(2,1)} %convert_element_type.40) | non-fusion elementwise | flops 2097152 | bytes 12582912 | tf_op jit(solution)/shard_map/mul | solution.py:16
  34.5 13.8 %broadcast_multiply_fusion = bf16[32,256,1024]{2,1,0:T(8,128)(2,1)} fusion(bf16[32,256,1024]{2,1,0:T(8,128)(2,1)} %param.9, bf16[256,1024]{1,0:T(8,128)(2,1)S(1)} %bitcast.52), kind=kLoop, calls=%fused_computation.8 | loop fusion | flops 8388608 | bytes 34078720 | tf_op jit(solution)/shard_map/mul | solution.py:17
  48.3 150.7 %all-to-all-done = bf16[8,128,4,1024]{3,1,2,0:T(8,128)(2,1)} async-done(((bf16[8,128,4,1024]{3,1,2,0:T(8,128)(2,1)}), bf16[8,128,4,1024]{3,1,2,0:T(8,128)(2,1)}, u32[]{:S(2)}, u32[]{:S(2)}) %all-to-all-start) | async-done | bytes 8388640 | tf_op jit(solution)/shard_map/all_to_all | solution.py:28
  199.0 0.0 copy-start.1
  199.0 8.3 %copy.22 = bf16[8,128,4,1024]{3,1,0,2:T(8,128)(2,1)} copy(bf16[8,128,4,1024]{3,1,2,0:T(8,128)(2,1)} %all-to-all-done) | data formatting | bytes 16777216 | tf_op jit(solution)/shard_map/all_to_all | solution.py:28
  207.3 0.0 copy-done.1
  207.3 0.0 copy-start
  207.3 12.3 %fusion.14 = f32[8,256,1024]{2,0,1:T(8,128)} fusion(bf16[8,256,1024]{2,1,0:T(8,128)(2,1)S(1)} %copy-done.1, bf16[1024,4,1024]{2,0,1:T(8,128)(2,1)} %bitcast.48), kind=kOutput, calls=%fused_computation.15 | convolution fusion | flops 4294967296 | bytes 14680064 | tf_op jit(solution)/shard_map/dot_general | solution.py:35
  219.6 0.0 copy-done
  219.6 10.8 %fusion.12 = f32[8,256,1024]{2,0,1:T(8,128)} fusion(bf16[8,256,1024]{2,1,0:T(8,128)(2,1)S(1)} %copy-done.1, bf16[1024,4,1024]{2,0,1:T(8,128)(2,1)S(1)} %bitcast.50), kind=kOutput, calls=%fused_computation.13 | convolution fusion | flops 4294967296 | bytes 14680064 | tf_op jit(solution)/shard_map/dot_general | solution.py:35
  230.4 0.0 slice-start
  230.4 0.0 slice-start.1
  230.4 10.6 %fusion.10 = f32[8,256,1024]{2,0,1:T(8,128)} fusion(bf16[8,256,1024]{2,1,0:T(8,128)(2,1)S(1)} %copy-done.1, bf16[1024,4,1024]{2,0,1:T(8,128)(2,1)S(1)} %bitcast.51), kind=kOutput, calls=%fused_computation.11 | convolution fusion | flops 4294967296 | bytes 14680064 | tf_op jit(solution)/shard_map/dot_general | solution.py:35
  241.0 0.0 slice-start.2
  241.0 0.0 slice-start.3
  241.0 12.2 %fusion.8 = f32[8,256,1024]{2,0,1:T(8,128)} fusion(bf16[8,256,1024]{2,1,0:T(8,128)(2,1)S(1)} %copy-done.1, bf16[1024,4,1024]{2,0,1:T(8,128)(2,1)} %bitcast.49), kind=kOutput, calls=%fused_computation.9 | convolution fusion | flops 4294967296 | bytes 14680064 | tf_op jit(solution)/shard_map/dot_general | solution.py:35
  253.2 0.0 slice-done
  253.2 0.0 slice-done.1
  253.2 0.0 slice-done.2
  253.2 0.0 slice-done.3
  253.2 42.1 %fusion.16 = f32[8,1,32]{2,0,1:T(8,128)S(1)} fusion(f32[8,256,1024]{2,0,1:T(8,128)} %fusion.14, bf16[32,256,1024]{2,1,0:T(8,128)(2,1)S(1)} %bitcast.47), kind=kOutput, calls=%fused_computation.22 | convolution fusion | flops 805306368 | bytes 25166848 | tf_op jit(solution)/shard_map/pcq,acq->pa/dot_general | solution.py:38
  295.4 32.5 %fusion.19 = f32[8,1,32]{2,0,1:T(8,128)S(1)} fusion(f32[8,256,1024]{2,0,1:T(8,128)} %fusion.12, bf16[32,256,1024]{2,1,0:T(8,128)(2,1)S(1)} %bitcast.47), kind=kOutput, calls=%fused_computation.23 | convolution fusion | flops 805306368 | bytes 25166848 | tf_op jit(solution)/shard_map/pcq,acq->pa/dot_general | solution.py:38
  327.8 32.2 %fusion.22 = f32[8,1,32]{2,0,1:T(8,128)S(1)} fusion(f32[8,256,1024]{2,0,1:T(8,128)} %fusion.10, bf16[32,256,1024]{2,1,0:T(8,128)(2,1)S(1)} %bitcast.47), kind=kOutput, calls=%fused_computation.24 | convolution fusion | flops 805306368 | bytes 25166848 | tf_op jit(solution)/shard_map/pcq,acq->pa/dot_general | solution.py:38
  360.0 0.0 copy-start.2
  360.0 32.3 %fusion.25 = f32[8,1,32]{2,0,1:T(8,128)S(1)} fusion(f32[8,256,1024]{2,0,1:T(8,128)} %fusion.8, bf16[32,256,1024]{2,1,0:T(8,128)(2,1)S(1)} %bitcast.47), kind=kOutput, calls=%fused_computation.25 | convolution fusion | flops 805306368 | bytes 25166848 | tf_op jit(solution)/shard_map/pcq,acq->pa/dot_general | solution.py:38
  392.3 57.6 %psum.7 = f32[8,4,32]{2,0,1:T(8,128)S(1)} all-reduce(f32[8,4,32]{2,0,1:T(8,128)S(1)} %pad_maximum_fusion), channel_id=1, replica_groups=mesh['occ'=2,'vir'=4,'aux'=4] {'vir','aux'}, use_global_device_ids=true, to_apply=%region_0.1 | all-reduce | flops 1024 | bytes 8192 | tf_op jit(solution)/shard_map/psum | solution.py:47
  450.0 0.0 copy-done.2
  450.0 0.6 copy.32
  (7 shorter events, 0.1 us)
Async XLA Ops:
  7.5 7.4 %copy-start.3 = (s32[8,2,8]{2,1,0:T(2,128)S(1)}, s32[8,2,8]{2,1,0:T(2,128)}, u32[]{:S(2)}) copy-start(s32[8,2,8]{2,1,0:T(2,128)} %param.8) | copy-start | bytes 1540
  7.5 191.4 %all-to-all-start = ((bf16[8,128,4,1024]{3,1,2,0:T(8,128)(2,1)}), bf16[8,128,4,1024]{3,1,2,0:T(8,128)(2,1)}, u32[]{:S(2)}, u32[]{:S(2)}) async-start(bf16[8,128,4,1024]{3,1,2,0:T(8,128)(2,1)} %stack.12), calls=%async_computation | async-start | bytes 16777216 | tf_op jit(solution)/shard_map/all_to_all | solution.py:28
  14.9 11.3 %copy-start.4 = (s32[2,8]{1,0:T(2,128)S(1)}, s32[2,8]{1,0:T(2,128)}, u32[]{:S(2)}) copy-start(s32[2,8]{1,0:T(2,128)} %param.10) | copy-start | bytes 196
  199.0 8.3 %copy-start.1 = (bf16[8,256,1024]{2,1,0:T(8,128)(2,1)S(1)}, bf16[8,256,1024]{2,1,0:T(8,128)(2,1)}, u32[]{:S(2)}) copy-start(bf16[8,256,1024]{2,1,0:T(8,128)(2,1)} %mul.25) | copy-start | bytes 12582916
  207.3 12.3 %copy-start = (bf16[8,128,4,1024]{3,1,0,2:T(8,128)(2,1)S(1)}, bf16[8,128,4,1024]{3,1,0,2:T(8,128)(2,1)}, u32[]{:S(2)}) copy-start(bf16[8,128,4,1024]{3,1,0,2:T(8,128)(2,1)} %copy.22) | copy-start | bytes 25165828
  230.4 22.8 %slice-start = ((s8[16777216]{0:T(1024)(128)(4,1)}), s8[4194304]{0:T(1024)(128)(4,1)S(1)}, s32[]{:S(2)}) async-start(s8[16777216]{0:T(1024)(128)(4,1)} %bitcast.46), calls=%async_computation.1 | async-start | bytes 8388608
  230.4 22.8 %slice-start.1 = ((s8[16777216]{0:T(1024)(128)(4,1)}), s8[4194304]{0:T(1024)(128)(4,1)S(1)}, s32[]{:S(2)}) async-start(s8[16777216]{0:T(1024)(128)(4,1)} %bitcast.46), calls=%async_computation.2 | async-start | bytes 8388608
  241.0 12.3 %slice-start.2 = ((s8[16777216]{0:T(1024)(128)(4,1)}), s8[4194304]{0:T(1024)(128)(4,1)S(1)}, s32[]{:S(2)}) async-start(s8[16777216]{0:T(1024)(128)(4,1)} %bitcast.46), calls=%async_computation.3 | async-start | bytes 8388608
  241.0 12.3 %slice-start.3 = ((s8[16777216]{0:T(1024)(128)(4,1)}), s8[4194304]{0:T(1024)(128)(4,1)S(1)}, s32[]{:S(2)}) async-start(s8[16777216]{0:T(1024)(128)(4,1)} %bitcast.46), calls=%async_computation.4 | async-start | bytes 8388608
  360.0 89.9 %copy-start.2 = (f32[8,4,32]{2,1,0:T(4,128)S(1)}, f32[8,4,32]{2,1,0:T(4,128)}, u32[]{:S(2)}) copy-start(f32[8,4,32]{2,1,0:T(4,128)} %param.13) | copy-start | bytes 12292
